TPU v7x, 256 devices: a 2x2x32 block of a 4x8x32 slice. The times are simulated.
256 devices in a mesh: member: 4 (over y, x), node: 64 (over z, core).
Axes of the slice: x: 2, y: 2, z: 32, core: 2. Of those that a mesh axis runs over, the one named last changes fastest.
The devices are a block of a 4x8x32 slice.
Arguments:
- conditioning: bfloat16 [168, 262144], P(None, ('member', 'node')), parts along dimension 1, may hold values from -6 to 6
- target_state: float32 [84, 262144], P(None, ('member', 'node')), parts along dimension 1, may hold values from -6 to 6
- noise_sample: float32 [84, 262144], P(None, ('member', 'node')), parts along dimension 1, may hold values from -6 to 6
- step_index: int32 [4], P('member'), parts along dimension 0, may hold values from 0 to 19
- mesh_features: float32 [3, 40960], P(None, 'node'), may hold values from -1 to 1
- edge_geometry: float32 [4, 262144], P(None, 'node'), may hold values from -6 to 6
- edge_slot: int32 [262144], P('node'), may hold values from 0 to 1023, as said below
- edge_receiver: int32 [262144], P('node'), may hold values from 0 to 639
- send_rows: int32 [4096, 16], P('node'), may hold values from 0 to 1023
- edge_count: int32 [64], P('node'), may hold values from 1503 to 4096, as said below
- embed_weight: bfloat16 [252, 512], replicated, may hold values from -0.375 to 0.375
- mesh_weight: float32 [3, 512], replicated, may hold values from -3.5 to 3.5
- geom_weight: float32 [4, 512], replicated, may hold values from -3 to 3
- sender_weight: bfloat16 [512, 512], P('node'), may hold values from -0.15625 to 0.15625
- edge_weight: bfloat16 [512, 512], P('node'), may hold values from -0.15625 to 0.15625
- receiver_weight: bfloat16 [512, 512], P('node'), may hold values from -0.15625 to 0.15625
- message_weight: bfloat16 [512, 512], P('node'), may hold values from -0.25 to 0.25
- node_weight: bfloat16 [1024, 512], P('node'), may hold values from -0.1875 to 0.1875
- output_weight: bfloat16 [512, 512], P('node'), may hold values from -0.25 to 0.25
- noise_weight: float32 [32, 512], replicated, may hold values from -1 to 1
- film_weight: bfloat16 [512, 2048], replicated, may hold values from -0.25 to 0.25
Outputs:
- mesh_latent: bfloat16 [40960, 2048], P('node', 'member'), parts along dimension 1
There are 4 independent parts, one for each index of `member`. A program takes and returns all parts, laid end to end along the dimension named above; an argument that names none is the same for every part. Nothing has to cross between parts.
Inputs may be any that keep to these rules, and one draw needn't show every extreme that they name: `edge_slot`: on each device, the live slots name every entry of its 64 * 16 list at least once, or as many distinct entries as there are live slots where these are fewer. `edge_count`: the counts sum to 64 * 2048 and one device has all 4096 slots live.
All inputs are finite; a program needn't handle non-finite values.
Results may differ from a plain program's by a relative error of at most 0.0071.
Values may be sent and summed in bfloat16 or wider, within the bound.
No kernel may reach another device: no remote copies, remote signals or barrier semaphores. Data moves between devices by JAX's collectives and lax.ppermute only.
A program may use at most 64 MiB of HBM per device.

v0:
```python
import jax
import jax.numpy as jnp
from jax import lax
from jax.sharding import PartitionSpec as P

STEPS = 20
sigma_top = 80.0
sigma_low = 0.03
rho_power = 7.0
norm_eps = 1e-05


def in_one_piece(arrays, axis, dim, along):
    widths = [a.shape[along] for a in arrays]
    both = jnp.concatenate(arrays, axis=along)
    out = lax.all_gather(both, axis, axis=dim, tiled=True)
    return tuple(jnp.split(out, [sum(widths[:k]) for k in range(1, len(widths))], axis=along))


def layer_norm(values):
    mean = jnp.mean(values, axis=-1, keepdims=True)
    centred = values - mean
    var = jnp.mean(centred * centred, axis=-1, keepdims=True)
    return centred * lax.rsqrt(var + norm_eps)


def embed_columns(inputs, embed_weight):
    product = lax.dot_general(
        inputs, embed_weight, (((0,), (0,)), ((), ())), preferred_element_type=jnp.float32
    )
    return jax.nn.silu(product).astype(jnp.bfloat16)


def per_device(
    conditioning,
    target_state,
    noise_sample,
    step_index,
    mesh_features,
    edge_geometry,
    edge_slot,
    edge_receiver,
    send_rows,
    edge_count,
    embed_weight,
    mesh_weight,
    geom_weight,
    sender_weight,
    edge_weight,
    receiver_weight,
    message_weight,
    node_weight,
    output_weight,
    noise_weight,
    film_weight,
):
    width = embed_weight.shape[1]
    freqs = noise_weight.shape[0] // 2
    steps_total = STEPS
    frac = step_index[0].astype(jnp.float32) / (steps_total - 1)
    upper = sigma_top ** (1.0 / rho_power)
    lower = sigma_low ** (1.0 / rho_power)
    sigma = (upper + frac * (lower - upper)) ** rho_power
    angle = 0.25 * jnp.log(sigma) * (jnp.arange(freqs, dtype=jnp.float32) + 1.0)
    fourier = jnp.concatenate([jnp.sin(angle), jnp.cos(angle)])[None, :]
    cond = jax.nn.silu(jnp.dot(fourier, noise_weight, precision=lax.Precision.HIGHEST)).astype(
        jnp.bfloat16
    )
    film = jnp.dot(cond, film_weight, preferred_element_type=jnp.float32)
    edge_scale = film[:, 0:width]
    edge_shift = film[:, width : 2 * width]
    node_scale = film[:, 2 * width : 3 * width]
    node_shift = film[:, 3 * width : 4 * width]
    full_sender, full_edge, full_recv, full_message, full_node, full_output = (
        *in_one_piece((sender_weight, edge_weight, receiver_weight, message_weight), "node", 0, 1),
        lax.all_gather(node_weight, "node", axis=0, tiled=True),
        lax.all_gather(output_weight, "node", axis=0, tiled=True),
    )
    noisy = ((target_state + sigma * noise_sample) / jnp.sqrt(sigma * sigma + 1.0)).astype(
        jnp.bfloat16
    )
    raw_local = jnp.concatenate([conditioning, noisy], axis=0)
    picked_rows = send_rows.reshape(-1)
    outgoing_inputs = raw_local[:, picked_rows]
    arrived = lax.all_to_all(outgoing_inputs, "node", split_axis=1, concat_axis=1, tiled=True)
    received = embed_columns(arrived, embed_weight)
    mesh_embed = jax.nn.silu(
        jnp.dot(mesh_features.T, mesh_weight, precision=lax.Precision.HIGHEST)
    ).astype(jnp.bfloat16)
    recv_proj = jnp.dot(mesh_embed, full_recv, preferred_element_type=jnp.float32).astype(
        jnp.bfloat16
    )
    mesh_count = mesh_embed.shape[0]
    slot_count = edge_slot.shape[0]
    block = min(512, slot_count)
    node_ids = jnp.arange(mesh_count, dtype=jnp.int32)
    count = edge_count[0]
    live_blocks = (count + block - 1) // block

    def add_block(index, total):
        start = (index * block).astype(jnp.int32)
        slots = lax.dynamic_slice_in_dim(edge_slot, start, block, 0)
        local_recv = lax.dynamic_slice_in_dim(edge_receiver, start, block, 0)
        geometry = lax.dynamic_slice_in_dim(edge_geometry, start, block, 1)
        embed_rows = jax.nn.silu(
            jnp.dot(geometry.T, geom_weight, precision=lax.Precision.HIGHEST)
        ).astype(jnp.bfloat16)
        one_hot = (local_recv[:, None] == node_ids[None, :]).astype(jnp.bfloat16)
        sender_rows = received[slots]
        pre = jnp.dot(embed_rows, full_edge, preferred_element_type=jnp.float32)
        pre = pre + jnp.dot(sender_rows, full_sender, preferred_element_type=jnp.float32)
        pre = pre + jnp.dot(one_hot, recv_proj, preferred_element_type=jnp.float32)
        hidden = jax.nn.silu(pre).astype(jnp.bfloat16)
        mixed = jnp.dot(hidden, full_message, preferred_element_type=jnp.float32)
        message = layer_norm(mixed) * (1.0 + edge_scale) + edge_shift
        live = start + jnp.arange(block, dtype=jnp.int32) < count
        message = jnp.where(live[:, None], message, 0.0).astype(jnp.bfloat16)
        return total + lax.dot_general(
            one_hot, message, (((0,), (0,)), ((), ())), preferred_element_type=jnp.float32
        )

    zeros_total = jnp.zeros((mesh_count, width), jnp.float32)
    summed = lax.fori_loop(0, live_blocks, add_block, zeros_total)
    gathered = summed.astype(jnp.bfloat16)
    joined = jnp.concatenate([mesh_embed, gathered], axis=1)
    update = jax.nn.silu(jnp.dot(joined, full_node, preferred_element_type=jnp.float32)).astype(
        jnp.bfloat16
    )
    result = jnp.dot(update, full_output, preferred_element_type=jnp.float32)
    return (
        mesh_embed.astype(jnp.float32) + layer_norm(result) * (1.0 + node_scale) + node_shift
    ).astype(jnp.bfloat16)


def solution(mesh):
    placed = (
        P(None, ("member", "node")),
        P(None, ("member", "node")),
        P(None, ("member", "node")),
        P("member"),
        P(None, "node"),
        P(None, "node"),
        P("node"),
        P("node"),
        P("node", None),
        P("node"),
        P(),
        P(),
        P(),
        P("node", None),
        P("node", None),
        P("node", None),
        P("node", None),
        P("node", None),
        P("node", None),
        P(),
        P(),
    )
    return jax.shard_map(
        per_device, mesh=mesh, in_specs=placed, out_specs=P("node", "member"), check_vma=False
    )
```

profile of v0, /device:TPU:1325, one launch (start us, length us, event | category | flops | bytes accessed | tf_op | source)
XLA Modules:
  0.0 331.0 jit_solution(2038196896726926414)
XLA Ops:
  6.6 1.5 pad_maximum_fusion.1
  10.8 5.0 %gather_fusion.1 = bf16[1024,252]{1,0:T(8,128)(2,1)} fusion(bf16[252,1024]{0,1:T(8,128)(2,1)S(1)} %pad_maximum_fusion, s32[1024]{0:T(1024)S(1)} %broadcast_clamp_fusion), kind=kCustom, calls=%fused_computation.1 | custom fusion | bytes 1036288 | tf_op jit(solution)/shard_map/gather | solution.py:84
  15.8 21.0 %all-to-all-start = ((bf16[252,64,16]{0,2,1:T(8,128)(2,1)}), bf16[252,64,16]{0,2,1:T(8,128)(2,1)S(1)}, u32[]{:S(2)}, u32[]{:S(2)}) async-start(bf16[252,64,16]{0,2,1:T(8,128)(2,1)} %bitcast.4), calls=%async_computation | async-start | bytes 1048576 | tf_op jit(solution)/shard_map/all_to_all | solution.py:85
  39.1 104.4 %all_gather.11 = bf16[512,512]{1,0:T(8,128)(2,1)} all-gather(bf16[8,512]{1,0:T(8,128)(2,1)S(1)} %copy-done.7), channel_id=1, replica_groups=mesh['member'=4,'node'=64] {'node'}, dimensions={0}, use_global_device_ids=true | all-gather | bytes 532480 | tf_op jit(solution)/shard_map/all_gather | solution.py:77
  143.5 2.2 multiply_convert_fusion.4
  146.5 1.8 multiply_convert_fusion.2
  148.4 2.6 fusion.41
  151.0 2.4 convolution_convert_fusion
  154.7 158.7 %while.11 = (s32[]{:T(128)}, f32[640,512]{1,0:T(8,128)}, s32[]{:T(128)}, s32[4096]{0:T(1024)}, s32[]{:T(128)}, /*index=5*/f32[4,4096]{1,0:T(4,128)}, f32[4,512]{...) while((s32[]{:T(128)}, f32[640,512]{1,0:T(8,128)}, ...), condition=%wide.region_3.4_spmd.clone, body=%wide.region_0.3_spmd.clone.sunk | while | flops 1496060416 | bytes 16973068 | solution.py:123
  154.7 1.9 multiply_convert_fusion.6
  156.7 1.4 fusion.84
  158.9 2.6 gather_fusion
  161.5 3.0 convolution_add_fusion.5
  165.2 3.7 %fusion.85 = (f32[512]{0:T(512)S(1)}, f32[512,512]{0,1:T(8,128)}) fusion(bf16[512,512]{1,0:T(8,128)(2,1)} %get-tuple-element.311, f32[512,512]{1,0:T(8,128)} %convolution_add_fusion.5, bf16[640,512]{1,0:T(8,128)(2,1)} %get-tuple-element.310, s32[512]{0:T(512)S(1)} %dynamic_slice.20), kind=kOutput, calls=%fused_computation.65.clone.1 | convolution fusion | flops 606141952 | bytes 3280896 | tf_op jit(solution)/shard_map/while/body/dot_general | solution.py:114
  169.0 1.4 multiply_reduce_fusion.3
  171.0 3.5 %convolution_add_fusion.6 = f32[640,512]{1,0:T(8,128)} fusion(f32[640,512]{1,0:T(8,128)} %get-tuple-element.281, s32[512]{0:T(512)S(1)} %dynamic_slice.20, f32[512,512]{0,1:T(8,128)} %get-tuple-element.259, f32[512]{0:T(512)S(1)} %bitcast.55, f32[512]{0:T(512)S(1)} %bitcast.54, f32[512]{0:T(512)S(1)} %add_rsqrt_fusion.3, ...), kind=kOutput, calls=%fused_computation.3.clone.1 | convolution fusion | flops 338100224 | bytes 3680768 | tf_op jit(solution)/shard_map/while/body/dot_general | solution.py:118
  174.5 1.9 multiply_convert_fusion.6
  176.5 1.4 fusion.84
  178.7 2.6 gather_fusion
  181.3 3.0 convolution_add_fusion.5
  185.1 3.7 %fusion.85 = (f32[512]{0:T(512)S(1)}, f32[512,512]{0,1:T(8,128)}) fusion(bf16[512,512]{1,0:T(8,128)(2,1)} %get-tuple-element.311, f32[512,512]{1,0:T(8,128)} %convolution_add_fusion.5, bf16[640,512]{1,0:T(8,128)(2,1)} %get-tuple-element.310, s32[512]{0:T(512)S(1)} %dynamic_slice.20), kind=kOutput, calls=%fused_computation.65.clone.1 | convolution fusion | flops 606141952 | bytes 3280896 | tf_op jit(solution)/shard_map/while/body/dot_general | solution.py:114
  190.9 3.5 %convolution_add_fusion.6 = f32[640,512]{1,0:T(8,128)} fusion(f32[640,512]{1,0:T(8,128)} %get-tuple-element.281, s32[512]{0:T(512)S(1)} %dynamic_slice.20, f32[512,512]{0,1:T(8,128)} %get-tuple-element.259, f32[512]{0:T(512)S(1)} %bitcast.55, f32[512]{0:T(512)S(1)} %bitcast.54, f32[512]{0:T(512)S(1)} %add_rsqrt_fusion.3, ...), kind=kOutput, calls=%fused_computation.3.clone.1 | convolution fusion | flops 338100224 | bytes 3680768 | tf_op jit(solution)/shard_map/while/body/dot_general | solution.py:118
  194.4 1.9 multiply_convert_fusion.6
  196.3 1.4 fusion.84
  198.5 2.6 gather_fusion
  201.2 3.0 convolution_add_fusion.5
  204.9 3.7 %fusion.85 = (f32[512]{0:T(512)S(1)}, f32[512,512]{0,1:T(8,128)}) fusion(bf16[512,512]{1,0:T(8,128)(2,1)} %get-tuple-element.311, f32[512,512]{1,0:T(8,128)} %convolution_add_fusion.5, bf16[640,512]{1,0:T(8,128)(2,1)} %get-tuple-element.310, s32[512]{0:T(512)S(1)} %dynamic_slice.20), kind=kOutput, calls=%fused_computation.65.clone.1 | convolution fusion | flops 606141952 | bytes 3280896 | tf_op jit(solution)/shard_map/while/body/dot_general | solution.py:114
  208.7 1.4 multiply_reduce_fusion.3
  210.7 3.5 %convolution_add_fusion.6 = f32[640,512]{1,0:T(8,128)} fusion(f32[640,512]{1,0:T(8,128)} %get-tuple-element.281, s32[512]{0:T(512)S(1)} %dynamic_slice.20, f32[512,512]{0,1:T(8,128)} %get-tuple-element.259, f32[512]{0:T(512)S(1)} %bitcast.55, f32[512]{0:T(512)S(1)} %bitcast.54, f32[512]{0:T(512)S(1)} %add_rsqrt_fusion.3, ...), kind=kOutput, calls=%fused_computation.3.clone.1 | convolution fusion | flops 338100224 | bytes 3680768 | tf_op jit(solution)/shard_map/while/body/dot_general | solution.py:118
  214.2 1.9 multiply_convert_fusion.6
  216.2 1.4 fusion.84
  218.4 2.6 gather_fusion
  221.0 3.0 convolution_add_fusion.5
  224.8 3.7 %fusion.85 = (f32[512]{0:T(512)S(1)}, f32[512,512]{0,1:T(8,128)}) fusion(bf16[512,512]{1,0:T(8,128)(2,1)} %get-tuple-element.311, f32[512,512]{1,0:T(8,128)} %convolution_add_fusion.5, bf16[640,512]{1,0:T(8,128)(2,1)} %get-tuple-element.310, s32[512]{0:T(512)S(1)} %dynamic_slice.20), kind=kOutput, calls=%fused_computation.65.clone.1 | convolution fusion | flops 606141952 | bytes 3280896 | tf_op jit(solution)/shard_map/while/body/dot_general | solution.py:114
  228.5 1.4 multiply_reduce_fusion.3
  230.5 3.5 %convolution_add_fusion.6 = f32[640,512]{1,0:T(8,128)} fusion(f32[640,512]{1,0:T(8,128)} %get-tuple-element.281, s32[512]{0:T(512)S(1)} %dynamic_slice.20, f32[512,512]{0,1:T(8,128)} %get-tuple-element.259, f32[512]{0:T(512)S(1)} %bitcast.55, f32[512]{0:T(512)S(1)} %bitcast.54, f32[512]{0:T(512)S(1)} %add_rsqrt_fusion.3, ...), kind=kOutput, calls=%fused_computation.3.clone.1 | convolution fusion | flops 338100224 | bytes 3680768 | tf_op jit(solution)/shard_map/while/body/dot_general | solution.py:118
  234.1 1.9 multiply_convert_fusion.6
  236.0 1.4 fusion.84
  238.2 2.6 gather_fusion
  240.8 3.0 convolution_add_fusion.5
  244.6 3.7 %fusion.85 = (f32[512]{0:T(512)S(1)}, f32[512,512]{0,1:T(8,128)}) fusion(bf16[512,512]{1,0:T(8,128)(2,1)} %get-tuple-element.311, f32[512,512]{1,0:T(8,128)} %convolution_add_fusion.5, bf16[640,512]{1,0:T(8,128)(2,1)} %get-tuple-element.310, s32[512]{0:T(512)S(1)} %dynamic_slice.20), kind=kOutput, calls=%fused_computation.65.clone.1 | convolution fusion | flops 606141952 | bytes 3280896 | tf_op jit(solution)/shard_map/while/body/dot_general | solution.py:114
  248.3 1.4 multiply_reduce_fusion.3
  250.4 3.5 %convolution_add_fusion.6 = f32[640,512]{1,0:T(8,128)} fusion(f32[640,512]{1,0:T(8,128)} %get-tuple-element.281, s32[512]{0:T(512)S(1)} %dynamic_slice.20, f32[512,512]{0,1:T(8,128)} %get-tuple-element.259, f32[512]{0:T(512)S(1)} %bitcast.55, f32[512]{0:T(512)S(1)} %bitcast.54, f32[512]{0:T(512)S(1)} %add_rsqrt_fusion.3, ...), kind=kOutput, calls=%fused_computation.3.clone.1 | convolution fusion | flops 338100224 | bytes 3680768 | tf_op jit(solution)/shard_map/while/body/dot_general | solution.py:118
  253.9 1.9 multiply_convert_fusion.6
  255.8 1.4 fusion.84
  258.1 2.6 gather_fusion
  260.7 3.0 convolution_add_fusion.5
  264.4 3.7 %fusion.85 = (f32[512]{0:T(512)S(1)}, f32[512,512]{0,1:T(8,128)}) fusion(bf16[512,512]{1,0:T(8,128)(2,1)} %get-tuple-element.311, f32[512,512]{1,0:T(8,128)} %convolution_add_fusion.5, bf16[640,512]{1,0:T(8,128)(2,1)} %get-tuple-element.310, s32[512]{0:T(512)S(1)} %dynamic_slice.20), kind=kOutput, calls=%fused_computation.65.clone.1 | convolution fusion | flops 606141952 | bytes 3280896 | tf_op jit(solution)/shard_map/while/body/dot_general | solution.py:114
  270.2 3.5 %convolution_add_fusion.6 = f32[640,512]{1,0:T(8,128)} fusion(f32[640,512]{1,0:T(8,128)} %get-tuple-element.281, s32[512]{0:T(512)S(1)} %dynamic_slice.20, f32[512,512]{0,1:T(8,128)} %get-tuple-element.259, f32[512]{0:T(512)S(1)} %bitcast.55, f32[512]{0:T(512)S(1)} %bitcast.54, f32[512]{0:T(512)S(1)} %add_rsqrt_fusion.3, ...), kind=kOutput, calls=%fused_computation.3.clone.1 | convolution fusion | flops 338100224 | bytes 3680768 | tf_op jit(solution)/shard_map/while/body/dot_general | solution.py:118
  273.7 1.9 multiply_convert_fusion.6
  275.7 1.4 fusion.84
  277.9 2.6 gather_fusion
  280.5 3.0 convolution_add_fusion.5
  284.3 3.7 %fusion.85 = (f32[512]{0:T(512)S(1)}, f32[512,512]{0,1:T(8,128)}) fusion(bf16[512,512]{1,0:T(8,128)(2,1)} %get-tuple-element.311, f32[512,512]{1,0:T(8,128)} %convolution_add_fusion.5, bf16[640,512]{1,0:T(8,128)(2,1)} %get-tuple-element.310, s32[512]{0:T(512)S(1)} %dynamic_slice.20), kind=kOutput, calls=%fused_computation.65.clone.1 | convolution fusion | flops 606141952 | bytes 3280896 | tf_op jit(solution)/shard_map/while/body/dot_general | solution.py:114
  290.0 3.5 %convolution_add_fusion.6 = f32[640,512]{1,0:T(8,128)} fusion(f32[640,512]{1,0:T(8,128)} %get-tuple-element.281, s32[512]{0:T(512)S(1)} %dynamic_slice.20, f32[512,512]{0,1:T(8,128)} %get-tuple-element.259, f32[512]{0:T(512)S(1)} %bitcast.55, f32[512]{0:T(512)S(1)} %bitcast.54, f32[512]{0:T(512)S(1)} %add_rsqrt_fusion.3, ...), kind=kOutput, calls=%fused_computation.3.clone.1 | convolution fusion | flops 338100224 | bytes 3680768 | tf_op jit(solution)/shard_map/while/body/dot_general | solution.py:118
  293.6 1.9 multiply_convert_fusion.6
  295.5 1.4 fusion.84
  297.7 2.6 gather_fusion
  300.3 3.0 convolution_add_fusion.5
  304.1 3.7 %fusion.85 = (f32[512]{0:T(512)S(1)}, f32[512,512]{0,1:T(8,128)}) fusion(bf16[512,512]{1,0:T(8,128)(2,1)} %get-tuple-element.311, f32[512,512]{1,0:T(8,128)} %convolution_add_fusion.5, bf16[640,512]{1,0:T(8,128)(2,1)} %get-tuple-element.310, s32[512]{0:T(512)S(1)} %dynamic_slice.20), kind=kOutput, calls=%fused_computation.65.clone.1 | convolution fusion | flops 606141952 | bytes 3280896 | tf_op jit(solution)/shard_map/while/body/dot_general | solution.py:114
  309.9 3.5 %convolution_add_fusion.6 = f32[640,512]{1,0:T(8,128)} fusion(f32[640,512]{1,0:T(8,128)} %get-tuple-element.281, s32[512]{0:T(512)S(1)} %dynamic_slice.20, f32[512,512]{0,1:T(8,128)} %get-tuple-element.259, f32[512]{0:T(512)S(1)} %bitcast.55, f32[512]{0:T(512)S(1)} %bitcast.54, f32[512]{0:T(512)S(1)} %add_rsqrt_fusion.3, ...), kind=kOutput, calls=%fused_computation.3.clone.1 | convolution fusion | flops 338100224 | bytes 3680768 | tf_op jit(solution)/shard_map/while/body/dot_general | solution.py:118
  313.4 2.4 copy.40
  315.8 3.9 %fusion.42 = (f32[640]{0:T(1024)S(1)}, f32[640,512]{0,1:T(8,128)S(1)}) fusion(bf16[512,512]{1,0:T(8,128)(2,1)} %all_gather.11, bf16[1024,512]{1,0:T(8,128)(2,1)} %all-gather.5.cloned.1.call-done, bf16[640,512]{0,1:T(8,128)(2,1)} %copy.40, bf16[640,512]{0,1:T(8,128)(2,1)} %multiply_convert_fusion.4), kind=kOutput, calls=%fused_computation.67 | convolution fusion | flops 1011219840 | bytes 4196864 | tf_op jit(solution)/shard_map/dot_general | solution.py:129
  322.0 2.2 copy.43
  (124 shorter events, 30.9 us)
Async XLA Ops:
  6.5 32.1 %copy-start = (bf16[512,2048]{1,0:T(8,128)(2,1)S(1)}, bf16[512,2048]{1,0:T(8,128)(2,1)}, u32[]{:S(2)}) copy-start(bf16[512,2048]{1,0:T(8,128)(2,1)} %param.43) | copy-start | bytes 6291460
  6.6 3.6 %copy-start.5 = (bf16[168,1024]{1,0:T(8,128)(2,1)S(1)}, bf16[168,1024]{1,0:T(8,128)(2,1)}, u32[]{:S(2)}) copy-start(bf16[168,1024]{1,0:T(8,128)(2,1)} %param.23) | copy-start | bytes 1032196
  6.6 3.9 %copy-start.8 = (s32[64,16]{0,1:T(8,128)S(1)}, s32[64,16]{0,1:T(8,128)}, u32[]{:S(2)}) copy-start(s32[64,16]{0,1:T(8,128)} %param.31) | copy-start | bytes 12292
  6.6 141.8 %all-gather.3.cloned.1.call-start = ((), (), s32[]{:S(2)}) async-start(), calls=%async_computation.1 | async-start | bytes 2129920 | tf_op jit(solution)/shard_map/all_gather | solution.py:16
  10.8 27.6 %copy-start.6 = (f32[32,512]{1,0:T(8,128)S(1)}, f32[32,512]{1,0:T(8,128)}, u32[]{:S(2)}) copy-start(f32[32,512]{1,0:T(8,128)} %param.42) | copy-start | bytes 196612
  15.8 129.9 %all-to-all-start = ((bf16[252,64,16]{0,2,1:T(8,128)(2,1)}), bf16[252,64,16]{0,2,1:T(8,128)(2,1)S(1)}, u32[]{:S(2)}, u32[]{:S(2)}) async-start(bf16[252,64,16]{0,2,1:T(8,128)(2,1)} %bitcast.4), calls=%async_computation | async-start | bytes 1048576 | tf_op jit(solution)/shard_map/all_to_all | solution.py:85
  36.8 2.3 copy-start.7
  36.8 279.0 %all-gather.5.cloned.1.call-start = ((), (), s32[]{:S(2)}) async-start(), calls=%async_computation.2 | async-start | bytes 1064960 | tf_op jit(solution)/shard_map/all_gather | solution.py:76
  38.7 104.8 %copy-start.9 = (f32[3,640]{1,0:T(4,128)S(1)}, f32[3,640]{1,0:T(4,128)}, u32[]{:S(2)}) copy-start(f32[3,640]{1,0:T(4,128)} %param.27) | copy-start | bytes 23044
  38.7 104.8 %copy-start.10 = (f32[3,512]{1,0:T(4,128)S(1)}, f32[3,512]{1,0:T(4,128)}, u32[]{:S(2)}) copy-start(f32[3,512]{1,0:T(4,128)} %param.34) | copy-start | bytes 18436
  145.7 0.8 copy-start.4
  148.4 2.6 copy-start.2
  151.0 3.7 %copy-start.11 = (f32[4,512]{1,0:T(4,128)S(1)}, f32[4,512]{1,0:T(4,128)}, u32[]{:S(2)}) copy-start(f32[4,512]{1,0:T(4,128)} %param.35) | copy-start | bytes 24580
  154.7 1.9 copy-start.1
  174.5 1.9 copy-start.1
  194.4 1.9 copy-start.1
  214.2 1.9 copy-start.1
  234.1 1.9 copy-start.1
  253.9 1.9 copy-start.1
  273.7 1.9 copy-start.1
  293.6 1.9 copy-start.1
  319.7 1.1 copy-start.3
Sparse Core Ops, SparseCore 0:
  9.2 137.0 all-gather.2
  148.2 123.3 all-gather.4
where the time goes:
time: 333 us; the launch traced here: 331 us
  matrix products  120 us (36%)
  blocking collectives  104 us (31%)
  local copies, waits for them, and re-layouts  42.7 us (13%)
  other arithmetic  26.8 us (8%)
  starting transfers between devices  21.1 us (6%)
  between operations  15.1 us (5%)
    all_gather x1, blocking collectives, per_device(): lax.all_gather(output_weight, 'node', axis=0, tiled=True)  104 us
    dot_general x8, matrix products, add_block(): mixed = jnp.dot(hidden, full_message, preferred_element_type=jnp.float32)  29.9 us
    dot_general x8, matrix products, add_block(): lax.dot_general(one_hot, message, (((0,), (0,)), ((), ())), preferred_ele...  28 us
    dot_general x8, matrix products, add_block(): jnp.dot(sender_rows, full_sender, preferred_element_type=jnp.float32)  24 us
    all_to_all x1, starting transfers between devices, per_device(): lax.all_to_all(outgoing_inputs, 'node', split_axis=1, concat_axis=1, tile...  21 us
    gather x8, local copies, waits for them, and re-layouts, add_block(): sender_rows = received[slots]  20.9 us
    dot_general x8, matrix products, add_block(): jnp.dot(geometry.T, geom_weight, precision=lax.Precision.HIGHEST)  15.4 us
    dot_general x8, matrix products, add_block(): pre = jnp.dot(embed_rows, full_edge, preferred_element_type=jnp.float32)  11.6 us
  transfers between devices with their start and end apart: 3, of which 0 were waited for; matrix products, arithmetic and copies ran while one was open for 54% of the time, Pallas kernels for 0%

commit v1 on v0

--- a/solution.py
+++ b/solution.py
@@ -54,6 +54,11 @@
     noise_weight,
     film_weight,
 ):
+
+    def _proceed_figure(patch):
+        formed = lax.all_to_all(jnp.stack([patch] * lax.axis_size("node")), "node", 0, 0)
+        return jnp.concatenate(formed, axis=0)
+
     width = embed_weight.shape[1]
     freqs = noise_weight.shape[0] // 2
     steps_total = STEPS
@@ -74,7 +79,7 @@
     full_sender, full_edge, full_recv, full_message, full_node, full_output = (
         *in_one_piece((sender_weight, edge_weight, receiver_weight, message_weight), "node", 0, 1),
         lax.all_gather(node_weight, "node", axis=0, tiled=True),
-        lax.all_gather(output_weight, "node", axis=0, tiled=True),
+        _proceed_figure(output_weight),
     )
     noisy = ((target_state + sigma * noise_sample) / jnp.sqrt(sigma * sigma + 1.0)).astype(
         jnp.bfloat16

time: 333 us -> 346 us (1.039)
  blocking collectives: 104 us -> 0 us
  waiting for transfers between devices: 0.81 us -> 93.4 us
  starting transfers between devices: 21.1 us -> 44 us
    all_gather x1 -> x0, blocking collectives: 104 us -> none  [per_device(): lax.all_gather(output_weight, 'node', axis=0, tiled=True)]
    all_to_all x1, waiting for transfers between devices: 0.01 us -> 48.1 us  [per_device(): lax.all_to_all(outgoing_inputs, 'node', split_axis=1, concat_axis=1, tile...]
    all_gather x1, waiting for transfers between devices: 0.02 us -> 44.6 us  [in_one_piece(): out = lax.all_gather(both, axis, axis=dim, tiled=True)]
    all_to_all x0 -> x1, starting transfers between devices: none -> 23 us  [_proceed_figure(): lax.all_to_all(jnp.stack([patch] * lax.axis_size('node')), 'node', 0, 0)]
  transfers between devices with their start and end apart: 3 -> 4, of which waited for: 0 -> 2; matrix products, arithmetic and copies ran while one was open for 54% -> 52% of each run, Pallas kernels for 0% -> 0%
where the time goes in v1:
time: 346 us; the launch traced here: 342 us
  matrix products  120 us (35%)
  waiting for transfers between devices  93.4 us (27%)
  starting transfers between devices  44 us (13%)
  local copies, waits for them, and re-layouts  42.8 us (12%)
  other arithmetic  26.8 us (8%)
  between operations  15.1 us (4%)
    all_to_all x1, waiting for transfers between devices, per_device(): lax.all_to_all(outgoing_inputs, 'node', split_axis=1, concat_axis=1, tile...  48.1 us
    all_gather x1, waiting for transfers between devices, in_one_piece(): out = lax.all_gather(both, axis, axis=dim, tiled=True)  44.6 us
    dot_general x8, matrix products, add_block(): mixed = jnp.dot(hidden, full_message, preferred_element_type=jnp.float32)  29.8 us
    dot_general x8, matrix products, add_block(): lax.dot_general(one_hot, message, (((0,), (0,)), ((), ())), preferred_ele...  28 us
    dot_general x8, matrix products, add_block(): jnp.dot(sender_rows, full_sender, preferred_element_type=jnp.float32)  23.8 us
    all_to_all x1, starting transfers between devices, _proceed_figure(): lax.all_to_all(jnp.stack([patch] * lax.axis_size('node')), 'node', 0, 0)  23 us
    all_to_all x1, starting transfers between devices, per_device(): lax.all_to_all(outgoing_inputs, 'node', split_axis=1, concat_axis=1, tile...  21 us
    gather x8, local copies, waits for them, and re-layouts, add_block(): sender_rows = received[slots]  21 us
  transfers between devices with their start and end apart: 4, of which 2 were waited for; matrix products, arithmetic and copies ran while one was open for 52% of the time, Pallas kernels for 0%

profile of v1, /device:TPU:1325, one launch (start us, length us, event | category | flops | bytes accessed | tf_op | source)
XLA Modules:
  0.0 341.9 jit_solution(12078315149600516588)
XLA Ops:
  6.6 1.5 pad_maximum_fusion.1
  10.8 5.0 %gather_fusion.1 = bf16[1024,252]{1,0:T(8,128)(2,1)} fusion(bf16[252,1024]{0,1:T(8,128)(2,1)S(1)} %pad_maximum_fusion, s32[1024]{0:T(1024)S(1)} %broadcast_clamp_fusion), kind=kCustom, calls=%fused_computation.1 | custom fusion | bytes 1036288 | tf_op jit(solution)/shard_map/gather | solution.py:89
  15.8 21.0 %all-to-all-start = ((bf16[252,64,16]{0,2,1:T(8,128)(2,1)}), bf16[252,64,16]{0,2,1:T(8,128)(2,1)S(1)}, u32[]{:S(2)}, u32[]{:S(2)}) async-start(bf16[252,64,16]{0,2,1:T(8,128)(2,1)} %bitcast.4), calls=%async_computation | async-start | bytes 1048576 | tf_op jit(solution)/shard_map/all_to_all | solution.py:90
  39.0 2.2 multiply_convert_fusion.4
  41.3 48.1 %all-to-all-done = bf16[252,64,16]{0,2,1:T(8,128)(2,1)S(1)} async-done(((bf16[252,64,16]{0,2,1:T(8,128)(2,1)}), bf16[252,64,16]{0,2,1:T(8,128)(2,1)S(1)}, u32[]{:S(2)}, u32[]{:S(2)}) %all-to-all-start) | async-done | bytes 516128 | tf_op jit(solution)/shard_map/all_to_all | solution.py:90
  90.3 23.0 %all-to-all-start.1 = ((bf16[64,8,512]{2,1,0:T(8,128)(2,1)}), bf16[64,8,512]{2,1,0:T(8,128)(2,1)}, u32[]{:S(2)}, u32[]{:S(2)}) async-start(bf16[64,8,512]{2,1,0:T(8,128)(2,1)} %stack.2), calls=%async_computation.1 | async-start | bytes 1048576 | tf_op jit(solution)/shard_map/all_to_all | solution.py:59
  113.2 1.8 multiply_convert_fusion.2
  115.1 44.6 %all-gather.3.cloned.1.call-done = bf16[512,2048]{1,0:T(8,128)(2,1)} async-done(((bf16[8,2048]{1,0:T(8,128)(2,1)}), bf16[512,2048]{1,0:T(8,128)(2,1)}) %all-gather.3.cloned.1.call-update) | async-done | bytes 2097168 | tf_op jit(solution)/shard_map/all_gather | solution.py:16
  159.7 2.6 fusion.42
  162.3 2.4 convolution_convert_fusion
  166.0 158.4 %while.11 = (s32[]{:T(128)}, f32[640,512]{1,0:T(8,128)}, s32[]{:T(128)}, s32[4096]{0:T(1024)}, s32[]{:T(128)}, /*index=5*/f32[4,4096]{1,0:T(4,128)}, f32[4,512]{...) while((s32[]{:T(128)}, f32[640,512]{1,0:T(8,128)}, ...), condition=%wide.region_3.4_spmd.clone, body=%wide.region_0.3_spmd.clone.sunk | while | flops 1496060416 | bytes 16973068 | solution.py:128
  166.0 1.9 multiply_convert_fusion.6
  167.9 1.4 fusion.84
  170.1 2.6 gather_fusion
  172.7 3.0 convolution_add_fusion.5
  176.5 3.7 %fusion.85 = (f32[512]{0:T(512)S(1)}, f32[512,512]{0,1:T(8,128)}) fusion(bf16[512,512]{1,0:T(8,128)(2,1)} %get-tuple-element.311, f32[512,512]{1,0:T(8,128)} %convolution_add_fusion.5, bf16[640,512]{1,0:T(8,128)(2,1)} %get-tuple-element.310, s32[512]{0:T(512)S(1)} %dynamic_slice.20), kind=kOutput, calls=%fused_computation.66.clone.1 | convolution fusion | flops 606141952 | bytes 3280896 | tf_op jit(solution)/shard_map/while/body/dot_general | solution.py:119
  180.2 1.4 multiply_reduce_fusion.3
  182.3 3.5 %convolution_add_fusion.6 = f32[640,512]{1,0:T(8,128)} fusion(f32[640,512]{1,0:T(8,128)} %get-tuple-element.281, s32[512]{0:T(512)S(1)} %dynamic_slice.20, f32[512,512]{0,1:T(8,128)} %get-tuple-element.259, f32[512]{0:T(512)S(1)} %bitcast.59, f32[512]{0:T(512)S(1)} %bitcast.58, f32[512]{0:T(512)S(1)} %add_rsqrt_fusion.3, ...), kind=kOutput, calls=%fused_computation.3.clone.1 | convolution fusion | flops 338100224 | bytes 3680768 | tf_op jit(solution)/shard_map/while/body/dot_general | solution.py:123
  185.8 1.9 multiply_convert_fusion.6
  187.7 1.4 fusion.84
  189.9 2.6 gather_fusion
  192.5 3.0 convolution_add_fusion.5
  196.3 3.7 %fusion.85 = (f32[512]{0:T(512)S(1)}, f32[512,512]{0,1:T(8,128)}) fusion(bf16[512,512]{1,0:T(8,128)(2,1)} %get-tuple-element.311, f32[512,512]{1,0:T(8,128)} %convolution_add_fusion.5, bf16[640,512]{1,0:T(8,128)(2,1)} %get-tuple-element.310, s32[512]{0:T(512)S(1)} %dynamic_slice.20), kind=kOutput, calls=%fused_computation.66.clone.1 | convolution fusion | flops 606141952 | bytes 3280896 | tf_op jit(solution)/shard_map/while/body/dot_general | solution.py:119
  202.1 3.5 %convolution_add_fusion.6 = f32[640,512]{1,0:T(8,128)} fusion(f32[640,512]{1,0:T(8,128)} %get-tuple-element.281, s32[512]{0:T(512)S(1)} %dynamic_slice.20, f32[512,512]{0,1:T(8,128)} %get-tuple-element.259, f32[512]{0:T(512)S(1)} %bitcast.59, f32[512]{0:T(512)S(1)} %bitcast.58, f32[512]{0:T(512)S(1)} %add_rsqrt_fusion.3, ...), kind=kOutput, calls=%fused_computation.3.clone.1 | convolution fusion | flops 338100224 | bytes 3680768 | tf_op jit(solution)/shard_map/while/body/dot_general | solution.py:123
  205.6 1.9 multiply_convert_fusion.6
  207.5 1.4 fusion.84
  209.7 2.6 gather_fusion
  212.3 3.0 convolution_add_fusion.5
  216.1 3.7 %fusion.85 = (f32[512]{0:T(512)S(1)}, f32[512,512]{0,1:T(8,128)}) fusion(bf16[512,512]{1,0:T(8,128)(2,1)} %get-tuple-element.311, f32[512,512]{1,0:T(8,128)} %convolution_add_fusion.5, bf16[640,512]{1,0:T(8,128)(2,1)} %get-tuple-element.310, s32[512]{0:T(512)S(1)} %dynamic_slice.20), kind=kOutput, calls=%fused_computation.66.clone.1 | convolution fusion | flops 606141952 | bytes 3280896 | tf_op jit(solution)/shard_map/while/body/dot_general | solution.py:119
  221.9 3.5 %convolution_add_fusion.6 = f32[640,512]{1,0:T(8,128)} fusion(f32[640,512]{1,0:T(8,128)} %get-tuple-element.281, s32[512]{0:T(512)S(1)} %dynamic_slice.20, f32[512,512]{0,1:T(8,128)} %get-tuple-element.259, f32[512]{0:T(512)S(1)} %bitcast.59, f32[512]{0:T(512)S(1)} %bitcast.58, f32[512]{0:T(512)S(1)} %add_rsqrt_fusion.3, ...), kind=kOutput, calls=%fused_computation.3.clone.1 | convolution fusion | flops 338100224 | bytes 3680768 | tf_op jit(solution)/shard_map/while/body/dot_general | solution.py:123
  225.4 1.9 multiply_convert_fusion.6
  227.3 1.4 fusion.84
  229.5 2.6 gather_fusion
  232.1 3.0 convolution_add_fusion.5
  235.9 3.7 %fusion.85 = (f32[512]{0:T(512)S(1)}, f32[512,512]{0,1:T(8,128)}) fusion(bf16[512,512]{1,0:T(8,128)(2,1)} %get-tuple-element.311, f32[512,512]{1,0:T(8,128)} %convolution_add_fusion.5, bf16[640,512]{1,0:T(8,128)(2,1)} %get-tuple-element.310, s32[512]{0:T(512)S(1)} %dynamic_slice.20), kind=kOutput, calls=%fused_computation.66.clone.1 | convolution fusion | flops 606141952 | bytes 3280896 | tf_op jit(solution)/shard_map/while/body/dot_general | solution.py:119
  241.7 3.5 %convolution_add_fusion.6 = f32[640,512]{1,0:T(8,128)} fusion(f32[640,512]{1,0:T(8,128)} %get-tuple-element.281, s32[512]{0:T(512)S(1)} %dynamic_slice.20, f32[512,512]{0,1:T(8,128)} %get-tuple-element.259, f32[512]{0:T(512)S(1)} %bitcast.59, f32[512]{0:T(512)S(1)} %bitcast.58, f32[512]{0:T(512)S(1)} %add_rsqrt_fusion.3, ...), kind=kOutput, calls=%fused_computation.3.clone.1 | convolution fusion | flops 338100224 | bytes 3680768 | tf_op jit(solution)/shard_map/while/body/dot_general | solution.py:123
  245.2 1.9 multiply_convert_fusion.6
  247.1 1.4 fusion.84
  249.3 2.6 gather_fusion
  251.9 3.0 convolution_add_fusion.5
  255.7 3.7 %fusion.85 = (f32[512]{0:T(512)S(1)}, f32[512,512]{0,1:T(8,128)}) fusion(bf16[512,512]{1,0:T(8,128)(2,1)} %get-tuple-element.311, f32[512,512]{1,0:T(8,128)} %convolution_add_fusion.5, bf16[640,512]{1,0:T(8,128)(2,1)} %get-tuple-element.310, s32[512]{0:T(512)S(1)} %dynamic_slice.20), kind=kOutput, calls=%fused_computation.66.clone.1 | convolution fusion | flops 606141952 | bytes 3280896 | tf_op jit(solution)/shard_map/while/body/dot_general | solution.py:119
  259.4 1.4 multiply_reduce_fusion.3
  261.5 3.5 %convolution_add_fusion.6 = f32[640,512]{1,0:T(8,128)} fusion(f32[640,512]{1,0:T(8,128)} %get-tuple-element.281, s32[512]{0:T(512)S(1)} %dynamic_slice.20, f32[512,512]{0,1:T(8,128)} %get-tuple-element.259, f32[512]{0:T(512)S(1)} %bitcast.59, f32[512]{0:T(512)S(1)} %bitcast.58, f32[512]{0:T(512)S(1)} %add_rsqrt_fusion.3, ...), kind=kOutput, calls=%fused_computation.3.clone.1 | convolution fusion | flops 338100224 | bytes 3680768 | tf_op jit(solution)/shard_map/while/body/dot_general | solution.py:123
  265.0 1.9 multiply_convert_fusion.6
  266.9 1.4 fusion.84
  269.1 2.6 gather_fusion
  271.7 3.0 convolution_add_fusion.5
  275.5 3.7 %fusion.85 = (f32[512]{0:T(512)S(1)}, f32[512,512]{0,1:T(8,128)}) fusion(bf16[512,512]{1,0:T(8,128)(2,1)} %get-tuple-element.311, f32[512,512]{1,0:T(8,128)} %convolution_add_fusion.5, bf16[640,512]{1,0:T(8,128)(2,1)} %get-tuple-element.310, s32[512]{0:T(512)S(1)} %dynamic_slice.20), kind=kOutput, calls=%fused_computation.66.clone.1 | convolution fusion | flops 606141952 | bytes 3280896 | tf_op jit(solution)/shard_map/while/body/dot_general | solution.py:119
  281.2 3.5 %convolution_add_fusion.6 = f32[640,512]{1,0:T(8,128)} fusion(f32[640,512]{1,0:T(8,128)} %get-tuple-element.281, s32[512]{0:T(512)S(1)} %dynamic_slice.20, f32[512,512]{0,1:T(8,128)} %get-tuple-element.259, f32[512]{0:T(512)S(1)} %bitcast.59, f32[512]{0:T(512)S(1)} %bitcast.58, f32[512]{0:T(512)S(1)} %add_rsqrt_fusion.3, ...), kind=kOutput, calls=%fused_computation.3.clone.1 | convolution fusion | flops 338100224 | bytes 3680768 | tf_op jit(solution)/shard_map/while/body/dot_general | solution.py:123
  284.8 1.9 multiply_convert_fusion.6
  286.7 1.4 fusion.84
  288.9 2.6 gather_fusion
  291.5 3.0 convolution_add_fusion.5
  295.3 3.7 %fusion.85 = (f32[512]{0:T(512)S(1)}, f32[512,512]{0,1:T(8,128)}) fusion(bf16[512,512]{1,0:T(8,128)(2,1)} %get-tuple-element.311, f32[512,512]{1,0:T(8,128)} %convolution_add_fusion.5, bf16[640,512]{1,0:T(8,128)(2,1)} %get-tuple-element.310, s32[512]{0:T(512)S(1)} %dynamic_slice.20), kind=kOutput, calls=%fused_computation.66.clone.1 | convolution fusion | flops 606141952 | bytes 3280896 | tf_op jit(solution)/shard_map/while/body/dot_general | solution.py:119
  301.0 3.5 %convolution_add_fusion.6 = f32[640,512]{1,0:T(8,128)} fusion(f32[640,512]{1,0:T(8,128)} %get-tuple-element.281, s32[512]{0:T(512)S(1)} %dynamic_slice.20, f32[512,512]{0,1:T(8,128)} %get-tuple-element.259, f32[512]{0:T(512)S(1)} %bitcast.59, f32[512]{0:T(512)S(1)} %bitcast.58, f32[512]{0:T(512)S(1)} %add_rsqrt_fusion.3, ...), kind=kOutput, calls=%fused_computation.3.clone.1 | convolution fusion | flops 338100224 | bytes 3680768 | tf_op jit(solution)/shard_map/while/body/dot_general | solution.py:123
  304.5 1.9 multiply_convert_fusion.6
  306.5 1.4 fusion.84
  308.7 2.6 gather_fusion
  311.3 3.0 convolution_add_fusion.5
  315.0 3.7 %fusion.85 = (f32[512]{0:T(512)S(1)}, f32[512,512]{0,1:T(8,128)}) fusion(bf16[512,512]{1,0:T(8,128)(2,1)} %get-tuple-element.311, f32[512,512]{1,0:T(8,128)} %convolution_add_fusion.5, bf16[640,512]{1,0:T(8,128)(2,1)} %get-tuple-element.310, s32[512]{0:T(512)S(1)} %dynamic_slice.20), kind=kOutput, calls=%fused_computation.66.clone.1 | convolution fusion | flops 606141952 | bytes 3280896 | tf_op jit(solution)/shard_map/while/body/dot_general | solution.py:119
  320.8 3.5 %convolution_add_fusion.6 = f32[640,512]{1,0:T(8,128)} fusion(f32[640,512]{1,0:T(8,128)} %get-tuple-element.281, s32[512]{0:T(512)S(1)} %dynamic_slice.20, f32[512,512]{0,1:T(8,128)} %get-tuple-element.259, f32[512]{0:T(512)S(1)} %bitcast.59, f32[512]{0:T(512)S(1)} %bitcast.58, f32[512]{0:T(512)S(1)} %add_rsqrt_fusion.3, ...), kind=kOutput, calls=%fused_computation.3.clone.1 | convolution fusion | flops 338100224 | bytes 3680768 | tf_op jit(solution)/shard_map/while/body/dot_general | solution.py:123
  324.3 2.4 copy.40
  326.7 3.9 %fusion.43 = (f32[640]{0:T(1024)S(1)}, f32[640,512]{0,1:T(8,128)S(1)}) fusion(bf16[64,8,512]{2,1,0:T(8,128)(2,1)} %all-to-all-done.1, bf16[1024,512]{1,0:T(8,128)(2,1)} %all-gather.5.cloned.1.call-done, bf16[640,512]{0,1:T(8,128)(2,1)} %copy.40, bf16[640,512]{0,1:T(8,128)(2,1)} %multiply_convert_fusion.4), kind=kOutput, calls=%fused_computation.68 | convolution fusion | flops 1011219840 | bytes 4196864 | tf_op jit(solution)/shard_map/dot_general | solution.py:134
  332.9 2.2 copy.43
  (126 shorter events, 33.7 us)
Async XLA Ops:
  6.5 32.1 %copy-start = (bf16[512,2048]{1,0:T(8,128)(2,1)S(1)}, bf16[512,2048]{1,0:T(8,128)(2,1)}, u32[]{:S(2)}) copy-start(bf16[512,2048]{1,0:T(8,128)(2,1)} %param.43) | copy-start | bytes 6291460
  6.6 3.6 %copy-start.5 = (bf16[168,1024]{1,0:T(8,128)(2,1)S(1)}, bf16[168,1024]{1,0:T(8,128)(2,1)}, u32[]{:S(2)}) copy-start(bf16[168,1024]{1,0:T(8,128)(2,1)} %param.23) | copy-start | bytes 1032196
  6.6 3.9 %copy-start.8 = (s32[64,16]{0,1:T(8,128)S(1)}, s32[64,16]{0,1:T(8,128)}, u32[]{:S(2)}) copy-start(s32[64,16]{0,1:T(8,128)} %param.31) | copy-start | bytes 12292
  6.6 153.1 %all-gather.3.cloned.1.call-start = ((), (), s32[]{:S(2)}) async-start(), calls=%async_computation.2 | async-start | bytes 2129920 | tf_op jit(solution)/shard_map/all_gather | solution.py:16
  10.8 27.6 %copy-start.6 = (f32[32,512]{1,0:T(8,128)S(1)}, f32[32,512]{1,0:T(8,128)}, u32[]{:S(2)}) copy-start(f32[32,512]{1,0:T(8,128)} %param.42) | copy-start | bytes 196612
  15.8 73.6 %all-to-all-start = ((bf16[252,64,16]{0,2,1:T(8,128)(2,1)}), bf16[252,64,16]{0,2,1:T(8,128)(2,1)S(1)}, u32[]{:S(2)}, u32[]{:S(2)}) async-start(bf16[252,64,16]{0,2,1:T(8,128)(2,1)} %bitcast.4), calls=%async_computation | async-start | bytes 1048576 | tf_op jit(solution)/shard_map/all_to_all | solution.py:90
  36.8 2.3 copy-start.9
  36.8 2.3 copy-start.10
  36.8 289.9 %all-gather.5.cloned.1.call-start = ((), (), s32[]{:S(2)}) async-start(), calls=%async_computation.3 | async-start | bytes 1064960 | tf_op jit(solution)/shard_map/all_gather | solution.py:81
  39.0 50.3 %copy-start.7 = (bf16[8,512]{1,0:T(8,128)(2,1)S(1)}, bf16[8,512]{1,0:T(8,128)(2,1)}, u32[]{:S(2)}) copy-start(bf16[8,512]{1,0:T(8,128)(2,1)} %param.41) | copy-start | bytes 24580
  89.4 23.9 %copy-start.4 = (bf16[252,64,16]{0,2,1:T(8,128)(2,1)}, bf16[252,64,16]{0,2,1:T(8,128)(2,1)S(1)}, u32[]{:S(2)}) copy-start(bf16[252,64,16]{0,2,1:T(8,128)(2,1)S(1)} %all-to-all-done) | copy-start | bytes 1548292
  90.3 236.5 %all-to-all-start.1 = ((bf16[64,8,512]{2,1,0:T(8,128)(2,1)}), bf16[64,8,512]{2,1,0:T(8,128)(2,1)}, u32[]{:S(2)}, u32[]{:S(2)}) async-start(bf16[64,8,512]{2,1,0:T(8,128)(2,1)} %stack.2), calls=%async_computation.1 | async-start | bytes 1048576 | tf_op jit(solution)/shard_map/all_to_all | solution.py:59
  159.6 2.6 copy-start.2
  162.3 3.7 %copy-start.11 = (f32[4,512]{1,0:T(4,128)S(1)}, f32[4,512]{1,0:T(4,128)}, u32[]{:S(2)}) copy-start(f32[4,512]{1,0:T(4,128)} %param.35) | copy-start | bytes 24580
  166.0 1.9 copy-start.1
  185.8 1.9 copy-start.1
  205.6 1.9 copy-start.1
  225.4 1.9 copy-start.1
  245.2 1.9 copy-start.1
  265.0 1.9 copy-start.1
  284.8 1.9 copy-start.1
  304.5 1.9 copy-start.1
  330.6 1.1 copy-start.3
Sparse Core Ops, SparseCore 0:
  9.2 150.4 all-gather.2
  161.5 123.6 all-gather.4
